TPU v7x, 32 devices: a whole 2x2x4 slice. The times are simulated.
32 devices in a mesh: band: 8 (over y, x, core), grid: 4 (over z).
Axes of the slice: x: 2, y: 2, z: 4, core: 2. Of those that a mesh axis runs over, the one named last changes fastest.
Arguments:
- orbitals: bfloat16 [64, 128, 128, 128], P('band', None, 'grid'), may hold values from -0.75 to 0.75
- occupations: float32 [64], P('band'), may hold values from 0 to 2
- rho_in: float32 [128, 128, 128], P('band', 'grid'), may hold values from 0.5 to 1.5
- hist_in: float32 [7, 128, 128, 128], P(None, 'band', 'grid'), may hold values from 0.5 to 1.5
- hist_res: float32 [7, 128, 128, 128], P(None, 'band', 'grid'), may hold values from -10 to 10
Outputs:
- rho_next: float32 [128, 128, 128], P('band', 'grid')
- v_hartree: float32 [128, 128, 128], P('band', 'grid')
All inputs are finite; a program needn't handle non-finite values.
Results may differ from a plain program's by a relative error of at most 0.0003.
Values sent between devices are 32-bit elements; how exact they have to be, the bound alone decides.
A program may use at most 64 MiB of HBM per device.

v0:
```python
import functools

import jax
import jax.numpy as jnp
import numpy as np
from jax import lax
from jax.experimental import pallas as pl
from jax.experimental.pallas import tpu as pltpu
from jax.sharding import PartitionSpec as P

beta_mix = 0.5
spacing = 0.2
MESH = pl.DeviceIdType.MESH
HIGH = lax.Precision.HIGHEST
F32 = jnp.float32


def cas_table(length):
    phases = np.outer(np.arange(length), np.arange(length)) % length
    angles = phases.astype(np.float64) * (2.0 * np.pi / length)
    return (np.cos(angles) + np.sin(angles)).astype(np.float32)


def dot(left, right):
    return jnp.dot(left, right, precision=HIGH, preferred_element_type=F32)


def swap_lane_groups(parts, width):
    count = len(parts)
    total = count * width
    group = lax.broadcasted_iota(jnp.int32, parts[0].shape, 1) // width
    results = []
    for j in range(count):
        result = parts[j]
        for i in range(count):
            if i != j:
                moved = pltpu.roll(parts[i], ((i - j) * width) % total, 1)
                result = jnp.where(group == i, moved, result)
        results.append(result)
    return results


def body(
    nb, ng,
    occ, orb_hbm, rho_hbm, hin_hbm, hres_hbm, cas_ref,
    rho_ref, pot_ref,
    orb, rin, hin, hres, other, own, pair_in, far_in, resn,
    gram_me, gram_b, gram_me2, gram_g, kern,
    zsend, zrecv, vsend, wrecv, wsend, vrecv, z2send, y2recv,
    load_sem, orb_sem,
    pair_s, pair_r, far_s, far_r, gb_s, gb_r, gg_s, gg_r,
    f1_s, f1_r, f2_s, f2_r, b2_s, b2_r, b1_s, b1_r,
):
    me = lax.axis_index("band")
    mg = lax.axis_index("grid")
    bands, rows, cols, n = orb.shape[1], orb.shape[2], orb.shape[3], orb.shape[4]
    hist = hin.shape[0]
    vecs = hist + 1
    chips = nb // 2
    chip, core = me // 2, me % 2
    partner = chip * 2 + (1 - core)
    quad = rows // ng
    width = n // ng
    qper = width // nb
    order = [d for d in range(chips // 2, 0, -1)] + [d for d in range(chips // 2 + 1, chips)] + [0]

    barrier = pltpu.get_barrier_semaphore()
    for k in range(1, nb):
        pl.semaphore_signal(barrier, inc=1, device_id=((me + k) % nb, mg), device_id_type=MESH)
    for k in range(1, ng):
        pl.semaphore_signal(barrier, inc=1, device_id=(me, (mg + k) % ng), device_id_type=MESH)

    def slab_of(t, mine):
        target = (chip + order[t]) % chips
        return target * 2 + (core if mine else 1 - core)

    orb_loads = []
    for t in range(chips):
        for mine in (False, True):
            s = slab_of(t, mine)
            c = pltpu.make_async_copy(
                orb_hbm.at[:, pl.ds(s * rows, rows)], orb.at[2 * t + mine], orb_sem.at[2 * t + mine]
            )
            c.start()
            orb_loads.append(c)
    loads = [
        pltpu.make_async_copy(hres_hbm, hres, load_sem.at[0]),
        pltpu.make_async_copy(hin_hbm, hin, load_sem.at[1]),
        pltpu.make_async_copy(rho_hbm, rin, load_sem.at[2]),
    ]
    for c in loads:
        c.start()

    def density(index, out):
        def row(a, carry):
            total = None
            for k in range(bands):
                o = orb[index, k, a].astype(F32)
                term = occ[k] * (o * o)
                total = term if total is None else total + term
            out[a] = total
            return carry

        lax.fori_loop(0, rows, row, 0)

    pair_copies, far_copies = [], []

    def finish(t):
        pair_copies[t].wait_recv()

        def row(a, carry):
            own[t, a] = own[t, a] + pair_in[t, a]
            return carry

        lax.fori_loop(0, rows, row, 0)
        if order[t]:
            target = (chip + order[t]) % chips
            c = pltpu.make_async_remote_copy(
                src_ref=own.at[t], dst_ref=far_in.at[t], send_sem=far_s.at[t], recv_sem=far_r.at[t],
                device_id=(target * 2 + core, mg), device_id_type=MESH,
            )
            c.start()
            far_copies.append(c)

    for t in range(chips):
        orb_loads[2 * t].wait()
        density(2 * t, other.at[t])
        if t == 0:
            pl.semaphore_wait(barrier, nb - 1 + ng - 1)
        c = pltpu.make_async_remote_copy(
            src_ref=other.at[t], dst_ref=pair_in.at[t], send_sem=pair_s.at[t], recv_sem=pair_r.at[t],
            device_id=(partner, mg), device_id_type=MESH,
        )
        c.start()
        pair_copies.append(c)
        orb_loads[2 * t + 1].wait()
        density(2 * t + 1, own.at[t])
        if t:
            finish(t - 1)
    finish(chips - 1)

    for c in loads:
        c.wait()
    tiles = cols // 8
    pairs = [(i, j) for i in range(hist) for j in range(i, hist)]

    def gram_row(a, accs):
        accs = list(accs)
        for s in range(tiles):
            vals = [hres[i, a, 8 * s:8 * s + 8, :] for i in range(hist)]
            for x, (i, j) in enumerate(pairs):
                accs[x] = accs[x] + vals[i] * vals[j]
        return tuple(accs)

    zero = jnp.zeros((8, n), F32)
    accs = lax.fori_loop(0, rows, gram_row, tuple(zero for _ in pairs))
    line = {p: jnp.sum(accs[x], axis=0, keepdims=True) for x, p in enumerate(pairs)}
    row_id = lax.broadcasted_iota(jnp.int32, (vecs, n), 0)
    col_id = lax.broadcasted_iota(jnp.int32, (vecs, n), 1)

    def stack(lines):
        result = jnp.zeros((vecs, n), F32)
        for i, l in enumerate(lines):
            result = jnp.where(row_id == i, l, result)
        return jnp.sum(result, axis=1, keepdims=True)

    gram = jnp.zeros((vecs, n), F32)
    for j in range(hist):
        column = stack([line[(min(i, j), max(i, j))] for i in range(hist)])
        gram = jnp.where(col_id == j, column, gram)

    def trial_row(a, carry):
        for m in range(hist):
            hin[m, a] = hin[m, a] + beta_mix * hres[m, a]
        return carry

    lax.fori_loop(0, rows, trial_row, 0)

    def freq2(positions):
        f = jnp.where(positions < n // 2, positions, positions - n)
        return f * f

    first = freq2(lax.broadcasted_iota(jnp.int32, (n, n), 0))
    lane = lax.broadcasted_iota(jnp.int32, (n, n), 1)
    last = freq2(mg * width + lane % width)
    cell = n * spacing
    for q in range(qper):
        middle = freq2((lane // width) * width + me * qper + q)
        squared = first + middle + last
        value = (cell * cell / np.pi) / jnp.maximum(squared, 1).astype(F32)
        kern[:, q * n:(q + 1) * n] = jnp.where(squared > 0, value, 0.0) * (1.0 / (n * n * n))

    for c in far_copies:
        c.wait_recv()

    def late_row(a, accs):
        accs = list(accs)
        total = own[chips - 1, a]
        for t in range(chips - 1):
            total = total + far_in[t, a]
        inp = rin[a]
        res = total - inp
        resn[a] = inp + beta_mix * res
        for s in range(tiles):
            r = res[8 * s:8 * s + 8, :]
            for i in range(hist):
                accs[i] = accs[i] + hres[i, a, 8 * s:8 * s + 8, :] * r
            accs[hist] = accs[hist] + r * r
        return tuple(accs)

    accs = lax.fori_loop(0, rows, late_row, tuple(zero for _ in range(vecs)))
    column = stack([jnp.sum(x, axis=0, keepdims=True) for x in accs])
    as_row = jnp.sum(jnp.where(row_id == col_id, column, 0.0), axis=0, keepdims=True)
    gram = jnp.where(col_id == hist, column, gram)
    gram = jnp.where(row_id == hist, as_row, gram)

    def sum_over(value, source, landing, send, recv, count, index, device_of):
        source[...] = value
        copies = []
        for k in range(1, count):
            c = pltpu.make_async_remote_copy(
                src_ref=source, dst_ref=landing.at[k], send_sem=send.at[k], recv_sem=recv.at[k],
                device_id=device_of((index + k) % count), device_id_type=MESH,
            )
            c.start()
            copies.append(c)
        for c in copies:
            c.wait_recv()
        landing[0] = value
        total = jnp.zeros_like(value)
        for k in range(count):
            total = total + landing[(index - k + count) % count]
        return total, copies

    sent = []
    gram, copies = sum_over(gram, gram_me, gram_b, gb_s, gb_r, nb, me, lambda x: (x, mg))
    sent += copies
    gram, copies = sum_over(gram, gram_me2, gram_g, gg_s, gg_r, ng, mg, lambda x: (me, x))
    sent += copies
    gram = gram * (1.0 / (n * n * n))

    system = jnp.where(col_id == vecs, 1.0, gram)
    for k in range(vecs):
        pivot_row = system[k:k + 1, :] / system[k:k + 1, k:k + 1]
        factor = jnp.where(row_id == k, 0.0, jnp.broadcast_to(system[:, k:k + 1], (vecs, n)))
        system = jnp.where(row_id == k, pivot_row, system - factor * pivot_row)
    solved = system[:, vecs:vecs + 1]
    weights = solved / jnp.sum(solved, axis=0, keepdims=True)
    wide = [jnp.broadcast_to(weights[m:m + 1, :], (cols, n)) for m in range(vecs)]

    def mix_row(a, carry):
        total = wide[hist] * resn[a]
        for m in range(hist):
            total = total + wide[m] * hin[m, a]
        rho_ref[a] = total
        return carry

    lax.fori_loop(0, rows, mix_row, 0)

    cas = cas_ref[...]

    def exchange(source, landing, send, recv, count, index, device_of):
        copies = []
        for k in range(1, count):
            to = (index + k) % count
            c = pltpu.make_async_remote_copy(
                src_ref=source.at[to], dst_ref=landing.at[index], send_sem=send.at[k],
                recv_sem=recv.at[k], device_id=device_of(to), device_id_type=MESH,
            )
            c.start()
            copies.append(c)
        landing[index] = source[index]
        for c in copies:
            c.wait_recv()
        return copies

    on_band = lambda x: (x, mg)
    on_grid = lambda x: (me, x)

    spec = dot(rho_ref[...].reshape(rows * cols, n), cas)
    chunk = quad * cols
    parts = swap_lane_groups([spec[i * chunk:(i + 1) * chunk] for i in range(ng)], width)
    for j in range(ng):
        zsend[j] = parts[j]
    sent += exchange(zsend, zrecv, f1_s, f1_r, ng, mg, on_grid)

    for u in range(quad):
        block = jnp.concatenate([zrecv[x, u * cols:(u + 1) * cols, :] for x in range(ng)], axis=0)
        spec = dot(cas, block)
        parts = swap_lane_groups([spec[j * width:(j + 1) * width] for j in range(ng)], width)
        for i in range(ng):
            vsend[:, :, i * quad + u, :] = parts[i].reshape(nb, qper, n)
    sent += exchange(vsend, wrecv, f2_s, f2_r, nb, me, on_band)

    for q in range(qper):
        block = wrecv[:, q].reshape(n, n)
        spec = dot(cas, block) * kern[:, q * n:(q + 1) * n]
        wsend[:, q] = dot(cas, spec).reshape(nb, rows, n)
    sent += exchange(wsend, vrecv, b2_s, b2_r, nb, me, on_band)

    for u in range(quad):
        parts = swap_lane_groups(
            [vrecv[:, :, i * quad + u, :].reshape(width, n) for i in range(ng)], width
        )
        back = dot(cas, jnp.concatenate(parts, axis=0))
        for x in range(ng):
            z2send[x, u * cols:(u + 1) * cols, :] = back[x * cols:(x + 1) * cols]
    sent += exchange(z2send, y2recv, b1_s, b1_r, ng, mg, on_grid)

    parts = swap_lane_groups([y2recv[j] for j in range(ng)], width)
    for i in range(ng):
        pot_ref[i * quad:(i + 1) * quad] = dot(parts[i], cas).reshape(quad, cols, n)

    for c in pair_copies + far_copies + sent:
        c.wait_send()


def local(nb, ng, orbitals, occupations, rho_in, hist_in, hist_res):
    bands = orbitals.shape[0]
    rows, cols, n = rho_in.shape
    hist = hist_in.shape[0]
    vecs = hist + 1
    chips = nb // 2
    width = n // ng
    qper = width // nb
    quad = rows // ng
    dma = pltpu.SemaphoreType.DMA
    vmem = lambda *shape: pltpu.VMEM(shape, F32)
    anywhere = pl.BlockSpec(memory_space=pl.ANY)
    block = jax.ShapeDtypeStruct((rows, cols, n), F32)
    return pl.pallas_call(
        functools.partial(body, nb, ng),
        out_shape=(block, block),
        in_specs=[pl.BlockSpec(memory_space=pltpu.SMEM)] + [anywhere] * 4 + [pl.BlockSpec(memory_space=pltpu.VMEM)],
        out_specs=(pl.BlockSpec(memory_space=pltpu.VMEM),) * 2,
        scratch_shapes=[
            pltpu.VMEM((nb, bands, rows, cols, n), orbitals.dtype),
            vmem(rows, cols, n),
            vmem(hist, rows, cols, n),
            vmem(hist, rows, cols, n),
            vmem(chips, rows, cols, n),
            vmem(chips, rows, cols, n),
            vmem(chips, rows, cols, n),
            vmem(chips, rows, cols, n),
            vmem(rows, cols, n),
            vmem(vecs, n),
            vmem(nb, vecs, n),
            vmem(vecs, n),
            vmem(ng, vecs, n),
            vmem(n, qper * n),
            vmem(ng, quad * cols, n),
            vmem(ng, quad * cols, n),
            vmem(nb, qper, rows, n),
            vmem(nb, qper, rows, n),
            vmem(nb, qper, rows, n),
            vmem(nb, qper, rows, n),
            vmem(ng, quad * cols, n),
            vmem(ng, quad * cols, n),
            dma((3,)), dma((nb,)),
            dma((chips,)), dma((chips,)), dma((chips,)), dma((chips,)),
            dma((nb,)), dma((nb,)), dma((ng,)), dma((ng,)),
            dma((ng,)), dma((ng,)), dma((nb,)), dma((nb,)),
            dma((nb,)), dma((nb,)), dma((ng,)), dma((ng,)),
        ],
        compiler_params=pltpu.CompilerParams(collective_id=0, has_side_effects=True, vmem_limit_bytes=48 * 1024 * 1024),
        name="density_mix_hartree",
    )(occupations, orbitals, rho_in, hist_in, hist_res, jnp.asarray(cas_table(n)))


def solution(mesh):
    return jax.shard_map(
        functools.partial(local, mesh.shape["band"], mesh.shape["grid"]),
        mesh=mesh,
        in_specs=(
            P("band", None, "grid", None),
            P("band"),
            P("band", "grid", None),
            P(None, "band", "grid", None),
            P(None, "band", "grid", None),
        ),
        out_specs=(P("band", "grid", None), P("band", "grid", None)),
        check_vma=False,
    )
```

profile of v0, /device:TPU:0, one launch (start us, length us, event | category | flops | bytes accessed | tf_op | source)
XLA Modules:
  0.0 62.9 jit_solution(7624885465194209670)
XLA Ops:
  0.6 0.0 copy-start
  0.6 1.5 %copy-done = f32[7,16,32,128]{3,2,1,0:T(8,128)S(1)} copy-done((f32[7,16,32,128]{3,2,1,0:T(8,128)S(1)}, f32[7,16,32,128]{3,2,1,0:T(8,128)}, u32[]{:S(2)}) %copy-start) | copy-done | bytes 1835032
  2.1 0.0 copy-start.1
  2.1 1.5 %copy-done.1 = f32[7,16,32,128]{3,2,1,0:T(8,128)S(1)} copy-done((f32[7,16,32,128]{3,2,1,0:T(8,128)S(1)}, f32[7,16,32,128]{3,2,1,0:T(8,128)}, u32[]{:S(2)}) %copy-start.1) | copy-done | bytes 1835032
  3.6 0.0 copy-start.2
  3.6 0.9 %copy-done.2 = f32[16,32,128]{2,1,0:T(8,128)S(1)} copy-done((f32[16,32,128]{2,1,0:T(8,128)S(1)}, f32[16,32,128]{2,1,0:T(8,128)}, u32[]{:S(2)}) %copy-start.2) | copy-done | bytes 262168
  4.6 0.0 copy-start.3
  4.6 0.8 %copy-done.3 = f32[128,128]{1,0:T(8,128)S(1)} copy-done((f32[128,128]{1,0:T(8,128)S(1)}, f32[128,128]{1,0:T(8,128)}, u32[]{:S(2)}) %copy-start.3) | copy-done | bytes 65560
  5.4 0.0 copy-start.4
  5.4 0.7 %copy-done.4 = f32[8]{0:T(128)S(1)} copy-done((f32[8]{0:T(128)S(1)}, f32[8]{0:T(128)}, u32[]{:S(2)}) %copy-start.4) | copy-done | bytes 56
  6.1 55.4 %density_mix_hartree.1 = (f32[16,32,128]{2,1,0:T(8,128)S(1)}, f32[16,32,128]{2,1,0:T(8,128)S(1)}) custom-call(f32[8]{0:T(128)S(1)} %copy-done.4, bf16[8,128,32,128]{3,2,1,0:T(8,128)(2,1)} %orb_hbm.1, f32[16,32,128]{2,1,0:T(8,128)S(1)} %copy-done.2, f32[7,16,32,128]{3,2,1,0:T(8,128)S(1)} %copy-done, f32[7,16,32,128]{3,2,1,0:T(8,128)S(1)} %copy-done.1, ...), custom_call_target="tpu_custom_call" | custom-call | tf_op jit(solution)/shard_map/density_mix_hartree/pallas_call | solution.py:331
  61.5 0.7 %copy.10 = f32[16,32,128]{2,1,0:T(8,128)} copy(f32[16,32,128]{2,1,0:T(8,128)S(1)} %get-tuple-element.4) | data formatting | bytes 524288
  62.2 0.7 %copy.11 = f32[16,32,128]{2,1,0:T(8,128)} copy(f32[16,32,128]{2,1,0:T(8,128)S(1)} %get-tuple-element.5) | data formatting | bytes 524288
Async XLA Ops:
  0.6 1.5 %copy-start = (f32[7,16,32,128]{3,2,1,0:T(8,128)S(1)}, f32[7,16,32,128]{3,2,1,0:T(8,128)}, u32[]{:S(2)}) copy-start(f32[7,16,32,128]{3,2,1,0:T(8,128)} %hin_hbm.1) | copy-start | bytes 5505028
  2.1 1.5 %copy-start.1 = (f32[7,16,32,128]{3,2,1,0:T(8,128)S(1)}, f32[7,16,32,128]{3,2,1,0:T(8,128)}, u32[]{:S(2)}) copy-start(f32[7,16,32,128]{3,2,1,0:T(8,128)} %hres_hbm.1) | copy-start | bytes 5505028
  3.6 0.9 %copy-start.2 = (f32[16,32,128]{2,1,0:T(8,128)S(1)}, f32[16,32,128]{2,1,0:T(8,128)}, u32[]{:S(2)}) copy-start(f32[16,32,128]{2,1,0:T(8,128)} %rho_hbm.1) | copy-start | bytes 786436
  4.6 0.8 %copy-start.3 = (f32[128,128]{1,0:T(8,128)S(1)}, f32[128,128]{1,0:T(8,128)}, u32[]{:S(2)}) copy-start(f32[128,128]{1,0:T(8,128)} %constant.2.clone.cas_ref) | copy-start | bytes 196612
  5.4 0.7 %copy-start.4 = (f32[8]{0:T(128)S(1)}, f32[8]{0:T(128)}, u32[]{:S(2)}) copy-start(f32[8]{0:T(128)} %occ.1) | copy-start | bytes 100
where the time goes:
time: 63.2 us; the launch traced here: 62.9 us
  Pallas kernels  55.4 us (88%)
  local copies, waits for them, and re-layouts  6.84 us (11%)
  between operations  0.65 us (1%)
    pallas_call x1, Pallas kernels, local(): pl.pallas_call(functools.partial(body, nb, ng), out_shape=(block, block),...  55.4 us
    unnamed x12, local copies, waits for them, and re-layouts  6.84 us

commit v1 on v0

--- a/solution.py
+++ b/solution.py
@@ -29,22 +29,25 @@
     count = len(parts)
     total = count * width
     group = lax.broadcasted_iota(jnp.int32, parts[0].shape, 1) // width
-    results = []
-    for j in range(count):
-        result = parts[j]
+    step = 1
+    while step < count:
+        odd = (group // step) % 2 == 1
+        mixed = []
         for i in range(count):
-            if i != j:
-                moved = pltpu.roll(parts[i], ((i - j) * width) % total, 1)
-                result = jnp.where(group == i, moved, result)
-        results.append(result)
-    return results
+            if (i // step) % 2 == 0:
+                mixed.append(jnp.where(odd, pltpu.roll(parts[i + step], step * width, 1), parts[i]))
+            else:
+                mixed.append(jnp.where(odd, parts[i], pltpu.roll(parts[i - step], total - step * width, 1)))
+        parts = mixed
+        step *= 2
+    return parts
 
 
 def body(
     nb, ng,
-    occ, orb_hbm, rho_hbm, hin_hbm, hres_hbm, cas_ref,
+    occ, orb_hbm, rho_hbm, hin_hbm, hres_hbm, cas_hbm,
     rho_ref, pot_ref,
-    orb, rin, hin, hres, other, own, pair_in, far_in, resn,
+    orb, rin, cas_ref, hin, hres, other, own, pair_in, far_in, relay_in, resn,
     gram_me, gram_b, gram_me2, gram_g, kern,
     zsend, zrecv, vsend, wrecv, wsend, vrecv, z2send, y2recv,
     load_sem, orb_sem,
@@ -59,9 +62,11 @@
     chips = nb // 2
     chip, core = me // 2, me % 2
     partner = chip * 2 + (1 - core)
-    quad = rows // ng
-    width = n // ng
+    chunks, width = cuts(nb, ng, rows, n)
+    groups = ng * chunks
+    quad = rows // groups
     qper = width // nb
+    square = chips == 4
     order = [d for d in range(chips // 2, 0, -1)] + [d for d in range(chips // 2 + 1, chips)] + [0]
 
     barrier = pltpu.get_barrier_semaphore()
@@ -70,8 +75,15 @@
     for k in range(1, ng):
         pl.semaphore_signal(barrier, inc=1, device_id=(me, (mg + k) % ng), device_id_type=MESH)
 
+    chip_y, chip_x = chip // 2, chip % 2
+    x_chip, y_chip = chip_y * 2 + 1 - chip_x, (1 - chip_y) * 2 + chip_x
+    opposite = (1 - chip_y) * 2 + 1 - chip_x
+
+    def target_of(t):
+        return (opposite, x_chip, y_chip, chip)[t] if square else (chip + order[t]) % chips
+
     def slab_of(t, mine):
-        target = (chip + order[t]) % chips
+        target = target_of(t)
         return target * 2 + (core if mine else 1 - core)
 
     orb_loads = []
@@ -87,6 +99,7 @@
         pltpu.make_async_copy(hres_hbm, hres, load_sem.at[0]),
         pltpu.make_async_copy(hin_hbm, hin, load_sem.at[1]),
         pltpu.make_async_copy(rho_hbm, rin, load_sem.at[2]),
+        pltpu.make_async_copy(cas_hbm, cas_ref, load_sem.at[3]),
     ]
     for c in loads:
         c.start()
@@ -113,14 +126,41 @@
             return carry
 
         lax.fori_loop(0, rows, row, 0)
-        if order[t]:
-            target = (chip + order[t]) % chips
-            c = pltpu.make_async_remote_copy(
-                src_ref=own.at[t], dst_ref=far_in.at[t], send_sem=far_s.at[t], recv_sem=far_r.at[t],
-                device_id=(target * 2 + core, mg), device_id_type=MESH,
-            )
-            c.start()
-            far_copies.append(c)
+        if square:
+            if t == 0:
+                far(own.at[0, :half], relay_in.at[0], 0, x_chip)
+                far(own.at[0, half:], relay_in.at[1], 1, y_chip)
+            if t == 1:
+                far(own.at[1, :half], far_in.at[0, :half], 2, x_chip)
+            if t == 2:
+                far(own.at[2, half:], far_in.at[1, half:], 3, y_chip)
+        elif order[t]:
+            far(own.at[t], far_in.at[t], t, target_of(t))
+
+    half = rows // 2
+
+    def far(source, landing, slot, target):
+        c = pltpu.make_async_remote_copy(
+            src_ref=source, dst_ref=landing, send_sem=far_s.at[slot], recv_sem=far_r.at[slot],
+            device_id=(target * 2 + core, mg), device_id_type=MESH,
+        )
+        c.start()
+        far_copies.append(c)
+
+    def relay():
+        def add(side, slab, base):
+            def row(a, carry):
+                own[slab, base + a] = own[slab, base + a] + relay_in[side, a]
+                return carry
+
+            lax.fori_loop(0, half, row, 0)
+
+        far_copies[1].wait_recv()
+        add(1, 1, half)
+        far(own.at[1, half:], far_in.at[0, half:], 4, x_chip)
+        far_copies[0].wait_recv()
+        add(0, 2, 0)
+        far(own.at[2, :half], far_in.at[1, :half], 5, y_chip)
 
     for t in range(chips):
         orb_loads[2 * t].wait()
@@ -138,6 +178,8 @@
         if t:
             finish(t - 1)
     finish(chips - 1)
+    if square:
+        relay()
 
     for c in loads:
         c.wait()
@@ -182,21 +224,21 @@
 
     first = freq2(lax.broadcasted_iota(jnp.int32, (n, n), 0))
     lane = lax.broadcasted_iota(jnp.int32, (n, n), 1)
-    last = freq2(mg * width + lane % width)
     cell = n * spacing
-    for q in range(qper):
+    for h, q in [(h, q) for h in range(chunks) for q in range(qper)]:
         middle = freq2((lane // width) * width + me * qper + q)
+        last = freq2((mg * chunks + h) * width + lane % width)
         squared = first + middle + last
         value = (cell * cell / np.pi) / jnp.maximum(squared, 1).astype(F32)
-        kern[:, q * n:(q + 1) * n] = jnp.where(squared > 0, value, 0.0) * (1.0 / (n * n * n))
-
-    for c in far_copies:
+        kern[h, q] = jnp.where(squared > 0, value, 0.0) * (1.0 / (n * n * n))
+
+    for c in far_copies[2 if square else 0:]:
         c.wait_recv()
 
     def late_row(a, accs):
         accs = list(accs)
         total = own[chips - 1, a]
-        for t in range(chips - 1):
+        for t in range(far_in.shape[0]):
             total = total + far_in[t, a]
         inp = rin[a]
         res = total - inp
@@ -270,49 +312,70 @@
             c.start()
             copies.append(c)
         landing[index] = source[index]
+        return copies
+
+    def arrive(copies):
         for c in copies:
             c.wait_recv()
-        return copies
+        sent.extend(copies)
 
     on_band = lambda x: (x, mg)
     on_grid = lambda x: (me, x)
+    span = range(chunks)
 
     spec = dot(rho_ref[...].reshape(rows * cols, n), cas)
     chunk = quad * cols
-    parts = swap_lane_groups([spec[i * chunk:(i + 1) * chunk] for i in range(ng)], width)
-    for j in range(ng):
-        zsend[j] = parts[j]
-    sent += exchange(zsend, zrecv, f1_s, f1_r, ng, mg, on_grid)
-
-    for u in range(quad):
-        block = jnp.concatenate([zrecv[x, u * cols:(u + 1) * cols, :] for x in range(ng)], axis=0)
-        spec = dot(cas, block)
-        parts = swap_lane_groups([spec[j * width:(j + 1) * width] for j in range(ng)], width)
-        for i in range(ng):
-            vsend[:, :, i * quad + u, :] = parts[i].reshape(nb, qper, n)
-    sent += exchange(vsend, wrecv, f2_s, f2_r, nb, me, on_band)
-
-    for q in range(qper):
-        block = wrecv[:, q].reshape(n, n)
-        spec = dot(cas, block) * kern[:, q * n:(q + 1) * n]
-        wsend[:, q] = dot(cas, spec).reshape(nb, rows, n)
-    sent += exchange(wsend, vrecv, b2_s, b2_r, nb, me, on_band)
-
-    for u in range(quad):
-        parts = swap_lane_groups(
-            [vrecv[:, :, i * quad + u, :].reshape(width, n) for i in range(ng)], width
-        )
-        back = dot(cas, jnp.concatenate(parts, axis=0))
+    parts = swap_lane_groups([spec[i * chunk:(i + 1) * chunk] for i in range(groups)], width)
+    flights = []
+    for h in span:
         for x in range(ng):
-            z2send[x, u * cols:(u + 1) * cols, :] = back[x * cols:(x + 1) * cols]
-    sent += exchange(z2send, y2recv, b1_s, b1_r, ng, mg, on_grid)
-
-    parts = swap_lane_groups([y2recv[j] for j in range(ng)], width)
-    for i in range(ng):
+            zsend[h, x] = parts[x * chunks + h]
+        flights.append(exchange(zsend.at[h], zrecv.at[h], f1_s.at[h], f1_r.at[h], ng, mg, on_grid))
+
+    nexts = []
+    for h in span:
+        arrive(flights[h])
+        for u in range(quad):
+            block = jnp.concatenate([zrecv[h, x, u * cols:(u + 1) * cols, :] for x in range(ng)], axis=0)
+            spec = dot(cas, block)
+            parts = swap_lane_groups([spec[j * width:(j + 1) * width] for j in range(groups)], width)
+            for i in range(groups):
+                vsend[h, :, :, i * quad + u, :] = parts[i].reshape(nb, qper, n)
+        nexts.append(exchange(vsend.at[h], wrecv.at[h], f2_s.at[h], f2_r.at[h], nb, me, on_band))
+
+    flights = []
+    for h in span:
+        arrive(nexts[h])
+        for q in range(qper):
+            spec = dot(cas, wrecv[h, :, q].reshape(n, n)) * kern[h, q]
+            wsend[h, :, q] = dot(cas, spec).reshape(nb, rows, n)
+        flights.append(exchange(wsend.at[h], vrecv.at[h], b2_s.at[h], b2_r.at[h], nb, me, on_band))
+
+    nexts = []
+    for h in span:
+        arrive(flights[h])
+        for u in range(quad):
+            parts = swap_lane_groups(
+                [vrecv[h, :, :, i * quad + u, :].reshape(width, n) for i in range(groups)], width
+            )
+            back = dot(cas, jnp.concatenate(parts, axis=0))
+            for x in range(ng):
+                z2send[h, x, u * cols:(u + 1) * cols, :] = back[x * cols:(x + 1) * cols]
+        nexts.append(exchange(z2send.at[h], y2recv.at[h], b1_s.at[h], b1_r.at[h], ng, mg, on_grid))
+
+    for h in span:
+        arrive(nexts[h])
+    parts = swap_lane_groups([y2recv[j % chunks, j // chunks] for j in range(groups)], width)
+    for i in range(groups):
         pot_ref[i * quad:(i + 1) * quad] = dot(parts[i], cas).reshape(quad, cols, n)
 
     for c in pair_copies + far_copies + sent:
         c.wait_send()
+
+
+def cuts(nb, ng, rows, n):
+    chunks = 2 if rows % (2 * ng) == 0 and n % (2 * ng * nb) == 0 else 1
+    return chunks, n // (ng * chunks)
 
 
 def local(nb, ng, orbitals, occupations, rho_in, hist_in, hist_res):
@@ -321,9 +384,10 @@
     hist = hist_in.shape[0]
     vecs = hist + 1
     chips = nb // 2
-    width = n // ng
+    chunks, width = cuts(nb, ng, rows, n)
     qper = width // nb
-    quad = rows // ng
+    quad = rows // (ng * chunks)
+    fars = 2 if chips == 4 else chips - 1
     dma = pltpu.SemaphoreType.DMA
     vmem = lambda *shape: pltpu.VMEM(shape, F32)
     anywhere = pl.BlockSpec(memory_space=pl.ANY)
@@ -331,38 +395,40 @@
     return pl.pallas_call(
         functools.partial(body, nb, ng),
         out_shape=(block, block),
-        in_specs=[pl.BlockSpec(memory_space=pltpu.SMEM)] + [anywhere] * 4 + [pl.BlockSpec(memory_space=pltpu.VMEM)],
+        in_specs=[pl.BlockSpec(memory_space=pltpu.SMEM)] + [anywhere] * 5,
         out_specs=(pl.BlockSpec(memory_space=pltpu.VMEM),) * 2,
         scratch_shapes=[
             pltpu.VMEM((nb, bands, rows, cols, n), orbitals.dtype),
             vmem(rows, cols, n),
+            vmem(n, n),
             vmem(hist, rows, cols, n),
             vmem(hist, rows, cols, n),
             vmem(chips, rows, cols, n),
             vmem(chips, rows, cols, n),
             vmem(chips, rows, cols, n),
-            vmem(chips, rows, cols, n),
+            vmem(fars, rows, cols, n),
+            vmem(2, rows // 2, cols, n),
             vmem(rows, cols, n),
             vmem(vecs, n),
             vmem(nb, vecs, n),
             vmem(vecs, n),
             vmem(ng, vecs, n),
-            vmem(n, qper * n),
-            vmem(ng, quad * cols, n),
-            vmem(ng, quad * cols, n),
-            vmem(nb, qper, rows, n),
-            vmem(nb, qper, rows, n),
-            vmem(nb, qper, rows, n),
-            vmem(nb, qper, rows, n),
-            vmem(ng, quad * cols, n),
-            vmem(ng, quad * cols, n),
-            dma((3,)), dma((nb,)),
-            dma((chips,)), dma((chips,)), dma((chips,)), dma((chips,)),
+            vmem(chunks, qper, n, n),
+            vmem(chunks, ng, quad * cols, n),
+            vmem(chunks, ng, quad * cols, n),
+            vmem(chunks, nb, qper, rows, n),
+            vmem(chunks, nb, qper, rows, n),
+            vmem(chunks, nb, qper, rows, n),
+            vmem(chunks, nb, qper, rows, n),
+            vmem(chunks, ng, quad * cols, n),
+            vmem(chunks, ng, quad * cols, n),
+            dma((4,)), dma((nb,)),
+            dma((chips,)), dma((chips,)), dma((max(chips, 6),)), dma((max(chips, 6),)),
             dma((nb,)), dma((nb,)), dma((ng,)), dma((ng,)),
-            dma((ng,)), dma((ng,)), dma((nb,)), dma((nb,)),
-            dma((nb,)), dma((nb,)), dma((ng,)), dma((ng,)),
+            dma((chunks, ng)), dma((chunks, ng)), dma((chunks, nb)), dma((chunks, nb)),
+            dma((chunks, nb)), dma((chunks, nb)), dma((chunks, ng)), dma((chunks, ng)),
         ],
-        compiler_params=pltpu.CompilerParams(collective_id=0, has_side_effects=True, vmem_limit_bytes=48 * 1024 * 1024),
+        compiler_params=pltpu.CompilerParams(collective_id=0, has_side_effects=True, vmem_limit_bytes=67043328),
         name="density_mix_hartree",
     )(occupations, orbitals, rho_in, hist_in, hist_res, jnp.asarray(cas_table(n)))
 

time: 63.2 us -> 55.1 us (0.87)
  Pallas kernels: 55.4 us -> 50.9 us
  local copies, waits for them, and re-layouts: 6.84 us -> 3.34 us
    pallas_call x1, Pallas kernels: 55.4 us -> 50.9 us  [local(): pl.pallas_call(functools.partial(body, nb, ng), out_shape=(block, block),...]
    unnamed x12 -> x2, local copies, waits for them, and re-layouts: 6.84 us -> 3.34 us
where the time goes in v1:
time: 55.1 us; the launch traced here: 54.9 us
  Pallas kernels  50.9 us (92%)
  local copies, waits for them, and re-layouts  3.34 us (6%)
  between operations  0.64 us (1%)
    pallas_call x1, Pallas kernels, local(): pl.pallas_call(functools.partial(body, nb, ng), out_shape=(block, block),...  50.9 us
    unnamed x2, local copies, waits for them, and re-layouts  3.34 us

profile of v1, /device:TPU:0, one launch (start us, length us, event | category | flops | bytes accessed | tf_op | source)
XLA Modules:
  0.0 54.9 jit_solution(8006457107511902416)
XLA Ops:
  0.6 50.9 %density_mix_hartree.1 = (f32[16,32,128]{2,1,0:T(8,128)}, f32[16,32,128]{2,1,0:T(8,128)}) custom-call(f32[8]{0:T(128)} %occ.1, bf16[8,128,32,128]{3,2,1,0:T(8,128)(2,1)} %orb_hbm.1, f32[16,32,128]{2,1,0:T(8,128)} %rho_hbm.1, f32[7,16,32,128]{3,2,1,0:T(8,128)} %hin_hbm.1, f32[7,16,32,128]{3,2,1,0:T(8,128)} %hres_hbm.1, f32[128,128]{1,0:T(8,128)} %constant.2.clone.cas_hbm), custom_call_target="tpu_custom_call" | custom-call | tf_op jit(solution)/shard_map/density_mix_hartree/pallas_call | solution.py:395
  51.5 1.7 %copy.10 = f32[16,32,128]{2,1,0:T(8,128)} copy(f32[16,32,128]{2,1,0:T(8,128)} %get-tuple-element.4) | data formatting | bytes 524288
  53.2 1.7 %copy.11 = f32[16,32,128]{2,1,0:T(8,128)} copy(f32[16,32,128]{2,1,0:T(8,128)} %get-tuple-element.5) | data formatting | bytes 524288

commit v2 on v1

--- a/solution.py
+++ b/solution.py
@@ -11,7 +11,6 @@
 beta_mix = 0.5
 spacing = 0.2
 MESH = pl.DeviceIdType.MESH
-HIGH = lax.Precision.HIGHEST
 F32 = jnp.float32
 
 
@@ -22,7 +21,12 @@
 
 
 def dot(left, right):
-    return jnp.dot(left, right, precision=HIGH, preferred_element_type=F32)
+    half = jnp.bfloat16
+    left_top, right_top = left.astype(half), right.astype(half)
+    left_rest = (left - left_top.astype(F32)).astype(half)
+    right_rest = (right - right_top.astype(F32)).astype(half)
+    times = lambda a, b: jnp.dot(a, b, preferred_element_type=F32)
+    return times(left_top, right_top) + (times(left_top, right_rest) + times(left_rest, right_top))
 
 
 def swap_lane_groups(parts, width):
@@ -392,7 +396,7 @@
     vmem = lambda *shape: pltpu.VMEM(shape, F32)
     anywhere = pl.BlockSpec(memory_space=pl.ANY)
     block = jax.ShapeDtypeStruct((rows, cols, n), F32)
-    return pl.pallas_call(
+    results = pl.pallas_call(
         functools.partial(body, nb, ng),
         out_shape=(block, block),
         in_specs=[pl.BlockSpec(memory_space=pltpu.SMEM)] + [anywhere] * 5,
@@ -432,6 +436,28 @@
         name="density_mix_hartree",
     )(occupations, orbitals, rho_in, hist_in, hist_res, jnp.asarray(cas_table(n)))
 
+    def hand_out(rho_from, pot_from, rho_to, pot_to, held, sem):
+        pairs = ((rho_from, rho_to), (pot_from, pot_to))
+        fetch = [pltpu.make_async_copy(a, held.at[x], sem.at[x]) for x, (a, b) in enumerate(pairs)]
+        put = [pltpu.make_async_copy(held.at[x], b, sem.at[2 + x]) for x, (a, b) in enumerate(pairs)]
+        for c in fetch:
+            c.start()
+        for x in range(2):
+            fetch[x].wait()
+            put[x].start()
+        for c in put:
+            c.wait()
+
+    return pl.pallas_call(
+        hand_out,
+        out_shape=(block, block),
+        in_specs=[anywhere] * 2,
+        out_specs=(anywhere,) * 2,
+        scratch_shapes=[vmem(2, rows, cols, n), dma((4,))],
+        compiler_params=pltpu.CompilerParams(vmem_limit_bytes=67043328),
+        name="hand_out",
+    )(*results)
+
 
 def solution(mesh):
     return jax.shard_map(

time: 55.1 us -> 52.8 us (0.958)
  local copies, waits for them, and re-layouts: 3.34 us -> 0 us
  Pallas kernels: 50.9 us -> 52 us
    unnamed x2 -> x0, local copies, waits for them, and re-layouts: 3.34 us -> none
    pallas_call x0 -> x1, Pallas kernels: none -> 1.77 us  [local(): pl.pallas_call(hand_out, out_shape=(block, block), in_specs=[anywhere] *...]
    pallas_call x1, Pallas kernels: 50.9 us -> 50.2 us  [local(): pl.pallas_call(functools.partial(body, nb, ng), out_shape=(block, block),...]
where the time goes in v2:
time: 52.8 us; the launch traced here: 52.6 us
  Pallas kernels  52 us (98%)
  between operations  0.64 us (1%)
    pallas_call x1, Pallas kernels, local(): pl.pallas_call(functools.partial(body, nb, ng), out_shape=(block, block),...  50.2 us
    pallas_call x1, Pallas kernels, local(): pl.pallas_call(hand_out, out_shape=(block, block), in_specs=[anywhere] *...  1.77 us

profile of v2, /device:TPU:0, one launch (start us, length us, event | category | flops | bytes accessed | tf_op | source)
XLA Modules:
  0.0 52.6 jit_solution(7969639782854842159)
XLA Ops:
  0.6 50.2 %density_mix_hartree.1 = (f32[16,32,128]{2,1,0:T(8,128)}, f32[16,32,128]{2,1,0:T(8,128)}) custom-call(f32[8]{0:T(128)} %occ.1, bf16[8,128,32,128]{3,2,1,0:T(8,128)(2,1)} %orb_hbm.1, f32[16,32,128]{2,1,0:T(8,128)} %rho_hbm.1, f32[7,16,32,128]{3,2,1,0:T(8,128)} %hin_hbm.1, f32[7,16,32,128]{3,2,1,0:T(8,128)} %hres_hbm.1, f32[128,128]{1,0:T(8,128)} %constant.2.clone.cas_hbm), custom_call_target="tpu_custom_call" | custom-call | tf_op jit(solution)/shard_map/density_mix_hartree/pallas_call | solution.py:399
  50.9 1.8 %hand_out.1 = (f32[16,32,128]{2,1,0:T(8,128)}, f32[16,32,128]{2,1,0:T(8,128)}) custom-call(f32[16,32,128]{2,1,0:T(8,128)} %get-tuple-element.4.rho_from, f32[16,32,128]{2,1,0:T(8,128)} %get-tuple-element.5.pot_from), custom_call_target="tpu_custom_call" | custom-call | tf_op jit(solution)/shard_map/hand_out/pallas_call | solution.py:451
